TPU v7x, 32 devices: a whole 2x2x4 slice. The times are simulated.
32 devices in a mesh: groups: 2 (over x), seq: 8 (over z, y), expert: 2 (over core).
Axes of the slice: x: 2, y: 2, z: 4, core: 2. Of those that a mesh axis runs over, the one named last changes fastest.
Arguments:
- residual: bfloat16 [8, 6144], P('groups', 'seq'), parts along dimension 0, may hold values from -27 to 27
- queries: bfloat16 [8, 6144], P('groups', 'expert'), parts along dimension 0, may hold values from -6 to 6
- new_entries: bfloat16 [2, 8, 1024], P(None, 'groups', 'expert'), parts along dimension 1, may hold values from -6 to 6
- kv_cache: bfloat16 [2, 1024, 16384], P(None, 'seq', ('groups', 'expert')), parts along dimension 2, may hold values from -6 to 6
- lengths: int32 [8], P('groups'), parts along dimension 0, may hold values from 128 to 2048, as said below
- routing: int32 [8, 2], P('groups'), parts along dimension 0, may hold values from 0 to 3, all different within a row
- w_out: bfloat16 [6144, 6144], P('expert', 'seq'), may hold values from -0.5 to 0.5
- norm_gain: bfloat16 [6144], replicated, may hold values from 0.5 to 1.5
- router: bfloat16 [6144, 4], replicated, may hold values from -0.078125 to 0.078125
- w_gate: bfloat16 [4, 6144, 1024], P('expert', None, 'seq'), may hold values from -0.078125 to 0.078125
- w_up: bfloat16 [4, 6144, 1024], P('expert', None, 'seq'), may hold values from -0.078125 to 0.078125
- w_down: bfloat16 [4, 1024, 6144], P('expert', 'seq'), may hold values from -0.75 to 0.75
Outputs:
- attended: bfloat16 [8, 6144], P('groups', 'seq'), parts along dimension 0
- expert_out: bfloat16 [8, 6144], P('groups', 'seq'), parts along dimension 0
There are 2 independent parts, one for each index of `groups`. A program takes and returns all parts, laid end to end along the dimension named above; an argument that names none is the same for every part. Nothing has to cross between parts.
Inputs may be any that keep to these rules, and one draw needn't show every extreme that they name: `lengths`: every draw has a request of exactly 2048 positions. `routing`: each request names two different experts.
All inputs are finite; a program needn't handle non-finite values.
Results may differ from a plain program's by a relative error of at most 0.02.
Values may be sent and summed in bfloat16 or wider, within the bound.
A program may use at most 128 MiB of HBM per device.

v0:
```python
import math
import jax
import jax.numpy as jnp
from jax import lax
from jax.sharding import PartitionSpec as P

H = 48
KVH = 8
HD = 128


def combined_all(value, axis, join):
    pieces = jax.tree.map(lambda part: lax.all_gather(part, axis), value)
    head = jax.tree.map(lambda part: part[0], pieces)
    tail = jax.tree.map(lambda part: part[1:], pieces)
    running, _ = lax.scan(lambda running, share: (join(running, share), None), head, tail)
    return running


def merge_parts(earlier, later):
    high_left, total_left, sum_left = earlier
    high_right, total_right, sum_right = later
    joined = jnp.maximum(high_left, high_right)
    scale_left = jnp.exp(high_left - joined)
    scale_right = jnp.exp(high_right - joined)
    return (
        joined,
        total_left * scale_left + total_right * scale_right,
        sum_left * scale_left[..., None] + sum_right * scale_right[..., None],
    )


def partial_attention(query_rows, relaid, positions, lengths, kv_count):
    requests = lengths.shape[0]
    per_group = H // KVH
    slot_count = relaid.shape[2] // requests
    query_heads = query_rows.reshape(requests, kv_count, per_group, HD)
    key_rows = relaid[0].reshape(kv_count, HD, slot_count, requests)
    value_rows = relaid[1].reshape(kv_count, HD, slot_count, requests)
    scores = jnp.einsum(
        "rgtd,gdpr->rgtp", query_heads, key_rows, preferred_element_type=jnp.float32
    ) * (1.0 / math.sqrt(HD))
    alive_mask = (positions[None, :] < lengths[:, None])[:, None, None, :]
    highest = jnp.max(jnp.where(alive_mask, scores, -1e30), axis=-1)
    weights = jnp.where(alive_mask, jnp.exp(scores - highest[..., None]), 0.0)
    summed = jnp.einsum(
        "rgtp,gdpr->rgtd",
        weights.astype(jnp.bfloat16),
        value_rows,
        preferred_element_type=jnp.float32,
    )
    return (highest, jnp.sum(weights, axis=-1), summed)


def on_device(
    residual,
    queries,
    new_entries,
    kv_cache,
    lengths,
    routing,
    w_out,
    norm_gain,
    router,
    w_gate,
    w_up,
    w_down,
):
    requests = lengths.shape[0]
    seq_count = lax.axis_size("seq")
    core_count = lax.axis_size("expert")
    seq_index = lax.axis_index("seq")
    core_index = lax.axis_index("expert")
    half_ctx = kv_cache.shape[2] // requests
    ctx_dev = half_ctx // seq_count
    own_heads = KVH // core_count
    relaid = lax.all_to_all(kv_cache, "seq", split_axis=2, concat_axis=1, tiled=True)
    positions = core_index * half_ctx + seq_index * ctx_dev + jnp.arange(ctx_dev, dtype=jnp.int32)
    all_queries = lax.all_gather(queries, "expert", axis=1, tiled=True)
    partials = partial_attention(all_queries, relaid, positions, lengths, KVH)
    merged = combined_all(partials, ("seq", "expert"), merge_parts)
    head_start = core_index * own_heads
    highest = lax.dynamic_slice_in_dim(merged[0], head_start, own_heads, 1)
    totals = lax.dynamic_slice_in_dim(merged[1], head_start, own_heads, 1)
    summed = lax.dynamic_slice_in_dim(merged[2], head_start, own_heads, 1)
    per_group = H // KVH
    query_heads = queries.reshape(requests, own_heads, per_group, HD)
    new_keys = new_entries[0].reshape(requests, own_heads, HD)
    new_values = new_entries[1].reshape(requests, own_heads, HD).astype(jnp.float32)
    own_score = jnp.einsum(
        "rgtd,rgd->rgt", query_heads, new_keys, preferred_element_type=jnp.float32
    ) * (1.0 / math.sqrt(HD))
    joined = jnp.maximum(highest, own_score)
    fade_old = jnp.exp(highest - joined)
    own_weight = jnp.exp(own_score - joined)
    numerator = summed * fade_old[..., None] + own_weight[..., None] * new_values[:, :, None, :]
    denominator = totals * fade_old + own_weight
    attn_rows = (
        (numerator / denominator[..., None])
        .reshape(requests, own_heads * per_group * HD)
        .astype(jnp.bfloat16)
    )
    head_terms = jnp.dot(attn_rows, w_out, preferred_element_type=jnp.float32)
    attended = (residual.astype(jnp.float32) + lax.psum(head_terms, "expert")).astype(jnp.bfloat16)
    gathered = lax.all_gather(attended, "seq", axis=1, tiled=True)
    widened = gathered.astype(jnp.float32)
    mean_square = jnp.mean(widened * widened, axis=-1, keepdims=True)
    normed = (widened * lax.rsqrt(mean_square + 1e-05) * norm_gain.astype(jnp.float32)).astype(
        jnp.bfloat16
    )
    logits = jnp.dot(normed, router, preferred_element_type=jnp.float32)
    expert_total = router.shape[1]
    picked = (
        routing[:, :, None] == jnp.arange(expert_total, dtype=jnp.int32)[None, None, :]
    ).astype(jnp.float32)
    chosen = jnp.sum(picked * logits[:, None, :], axis=-1)
    first_share = jax.nn.sigmoid(chosen[:, 0] - chosen[:, 1])
    shares = jnp.stack([first_share, 1.0 - first_share], axis=-1)
    combine = jnp.sum(picked * shares[:, :, None], axis=1)
    local_ids = core_index * w_gate.shape[0] + jnp.arange(w_gate.shape[0], dtype=jnp.int32)
    select = (jnp.arange(expert_total, dtype=jnp.int32)[:, None] == local_ids[None, :]).astype(
        jnp.float32
    )
    local_share = jnp.sum(combine[:, :, None] * select[None, :, :], axis=1)
    gate_proj = jnp.einsum("rd,edf->ref", normed, w_gate, preferred_element_type=jnp.float32)
    upward = jnp.einsum("rd,edf->ref", normed, w_up, preferred_element_type=jnp.float32)
    activation = (jax.nn.silu(gate_proj) * upward * local_share[:, :, None]).astype(jnp.bfloat16)
    expert_terms = jnp.einsum("ref,efd->rd", activation, w_down, preferred_element_type=jnp.float32)
    reduced = lax.psum_scatter(expert_terms, "seq", scatter_dimension=1, tiled=True)
    expert_out = lax.psum(reduced, "expert").astype(jnp.bfloat16)
    return (attended, expert_out)


def solution(mesh):
    in_specs = (
        P("groups", "seq"),
        P("groups", "expert"),
        P(None, "groups", "expert"),
        P(None, "seq", ("groups", "expert")),
        P("groups"),
        P("groups", None),
        P("expert", "seq"),
        P(),
        P(),
        P("expert", None, "seq"),
        P("expert", None, "seq"),
        P("expert", "seq", None),
    )
    out_specs = (P("groups", "seq"), P("groups", "seq"))
    return jax.shard_map(
        on_device, mesh=mesh, in_specs=in_specs, out_specs=out_specs, check_vma=False
    )
```

profile of v0, /device:TPU:0, one launch (start us, length us, event | category | flops | bytes accessed | tf_op | source)
XLA Modules:
  0.0 286.1 jit_solution(10244432440107724800)
XLA Ops:
  7.2 6.3 %copy.89 = bf16[2,128,4096]{1,0,2:T(2,128)(2,1)} copy(bf16[2,128,4096]{2,1,0:T(8,128)(2,1)} %param.17) | data formatting | bytes 4194304 | tf_op args[3]
  13.5 7.4 %all-to-all-start = ((bf16[2,128,4096]{1,0,2:T(2,128)(2,1)}), bf16[2,128,4096]{1,0,2:T(2,128)(2,1)}, u32[]{:S(2)}, u32[]{:S(2)}) async-start(bf16[2,128,4096]{1,0,2:T(2,128)(2,1)} %copy.89), calls=%async_computation | async-start | bytes 4194304 | tf_op jit(solution)/shard_map/all_to_all | solution.py:77
  21.0 1.8 all_gather.24
  23.0 46.3 %all-to-all-done = bf16[2,128,4096]{1,0,2:T(2,128)(2,1)} async-done(((bf16[2,128,4096]{1,0,2:T(2,128)(2,1)}), bf16[2,128,4096]{1,0,2:T(2,128)(2,1)}, u32[]{:S(2)}, u32[]{:S(2)}) %all-to-all-start) | async-done | bytes 2097184 | tf_op jit(solution)/shard_map/all_to_all | solution.py:77
  69.3 1.9 copy.90
  75.6 20.3 %all-gather.1 = f32[64,8,6]{2,1,0:T(8,128)S(1)} all-gather(f32[4,8,6]{2,1,0:T(8,128)S(1)} %fusion.10), channel_id=3, replica_groups=mesh['groups'=2,'seq'=8,'expert'=2] {'seq','expert'}, dimensions={0}, use_global_device_ids=true | all-gather | bytes 13056 | tf_op jit(solution)/shard_map/all_gather | solution.py:13
  95.9 18.6 %all-gather = f32[64,8,6]{2,1,0:T(8,128)S(1)} all-gather(f32[4,8,6]{2,1,0:T(8,128)S(1)} %get-tuple-element.106), channel_id=2, replica_groups=mesh['groups'=2,'seq'=8,'expert'=2] {'seq','expert'}, dimensions={0}, use_global_device_ids=true | all-gather | bytes 13056 | tf_op jit(solution)/shard_map/all_gather | solution.py:13
  115.8 1.1 copy.102
  117.0 1.4 copy.101
  119.2 0.9 slice.60
  120.2 2.6 slice.63
  122.7 30.3 %while.14 = (s32[]{:T(128)}, f32[4,8,6]{1,0,2:T(4,128)S(1)}, f32[4,8,6]{1,0,2:T(4,128)S(1)}, f32[4,8,6,128]{3,2,1,0:T(8,128)S(1)}, f32[15,4,8,6]{2,1,3,0:T(4,128...) while((s32[]{:T(128)}, f32[4,8,6]{1,0,2:T(4,128)S(1)}, ...), condition=%wide.region_3.4_spmd, body=%wide.region_2.3_spmd.sunk | while | flops 74882 | bytes 502365 | solution.py:16
  123.7 0.9 constant_dynamic-slice_fusion.2
  125.7 0.9 constant_dynamic-slice_fusion.2
  127.7 0.9 constant_dynamic-slice_fusion.2
  129.8 0.9 constant_dynamic-slice_fusion.2
  131.8 0.9 constant_dynamic-slice_fusion.2
  133.8 0.9 constant_dynamic-slice_fusion.2
  135.8 0.9 constant_dynamic-slice_fusion.2
  137.9 0.9 constant_dynamic-slice_fusion.2
  139.9 0.9 constant_dynamic-slice_fusion.2
  141.9 0.9 constant_dynamic-slice_fusion.2
  143.9 0.9 constant_dynamic-slice_fusion.2
  152.0 0.9 constant_dynamic-slice_fusion.2
  154.9 3.1 %fusion.36 = f32[4,768]{1,0:T(4,128)S(1)} fusion(bf16[4,3072]{1,0:T(4,128)(2,1)S(1)} %convert_element_type.53, bf16[3072,768]{1,0:T(8,128)(2,1)} %param.20), kind=kOutput, calls=%fused_computation.63 | convolution fusion | flops 18874368 | bytes 4755456 | tf_op jit(solution)/shard_map/dot_general | solution.py:103
  158.0 3.5 %psum.14 = f32[4,768]{1,0:T(4,128)S(1)} all-reduce(f32[4,768]{1,0:T(4,128)S(1)} %fusion.36), channel_id=1, replica_groups=mesh['groups'=2,'seq'=8,'expert'=2] {'expert'}, use_global_device_ids=true, to_apply=%region_4.5 | all-reduce | flops 3072 | bytes 24576 | tf_op jit(solution)/shard_map/psum | solution.py:104
  161.5 30.8 %all_gather.31 = bf16[4,6144]{1,0:T(4,128)(2,1)S(1)} all-gather(bf16[4,768]{1,0:T(4,128)(2,1)S(1)} %add_convert_fusion), channel_id=1, replica_groups=mesh['groups'=2,'seq'=8,'expert'=2] {'seq'}, dimensions={1}, use_global_device_ids=true | all-gather | bytes 55296 | tf_op jit(solution)/shard_map/all_gather | solution.py:105
  193.0 2.4 fusion.20
  195.5 5.8 %convolution_bitcast_fusion = f32[6144,4]{1,0:T(8,128)} fusion(bf16[2,128,6144]{2,1,0:T(8,128)(2,1)S(1)} %copy-done, bf16[2,6144,128]{2,1,0:T(8,128)(2,1)} %param.24, bf16[4,6144]{1,0:T(4,128)(2,1)S(1)} %fusion.13, f32[4,2,128]{2,0,1:T(4,128)S(1)} %fusion.20, f32[4,2]{0,1:T(2,128)S(1)} %multiply_reduce_fusion), kind=kOutput, calls=%fused_computation.10 | convolution fusion | flops 25172992 | bytes 6443040 | tf_op jit(solution)/shard_map/ref,efd->rd/dot_general | solution.py:128
  201.3 72.9 %reduce-scatter.4.cloned.1.call-done = f32[768,4]{1,0:T(8,128)} async-done(((f32[6144,4]{1,0:T(8,128)}), f32[768,4]{1,0:T(8,128)}) %reduce-scatter.4.cloned.1.call-update) | async-done | bytes 12304
  274.2 1.1 copy.117
  275.4 3.9 %psum.15 = bf16[4,768]{1,0:T(4,128)(2,1)} all-reduce(f32[4,768]{1,0:T(4,128)S(1)} %copy.117), channel_id=1, replica_groups=mesh['groups'=2,'seq'=8,'expert'=2] {'expert'}, use_global_device_ids=true, to_apply=%region_10.11 | all-reduce | flops 3072 | bytes 18432 | tf_op jit(solution)/shard_map/psum | solution.py:130
  (126 shorter events, 28.7 us)
Async XLA Ops:
  7.2 188.3 %copy-start = (bf16[2,128,6144]{2,1,0:T(8,128)(2,1)S(1)}, bf16[2,128,6144]{2,1,0:T(8,128)(2,1)}, u32[]{:S(2)}) copy-start(bf16[2,128,6144]{2,1,0:T(8,128)(2,1)} %param.25) | copy-start | bytes 9437188
  13.5 7.5 %copy-start.1 = (bf16[4,3072]{1,0:T(4,128)(2,1)S(1)}, bf16[4,3072]{1,0:T(4,128)(2,1)}, u32[]{:S(2)}) copy-start(bf16[4,3072]{1,0:T(4,128)(2,1)} %param.15) | copy-start | bytes 73732
  13.5 9.4 %copy-start.9 = (s32[4]{0:T(128)S(1)}, s32[4]{0:T(128)}, u32[]{:S(2)}) copy-start(s32[4]{0:T(128)} %param.18) | copy-start | bytes 52
  13.5 55.8 %all-to-all-start = ((bf16[2,128,4096]{1,0,2:T(2,128)(2,1)}), bf16[2,128,4096]{1,0,2:T(2,128)(2,1)}, u32[]{:S(2)}, u32[]{:S(2)}) async-start(bf16[2,128,4096]{1,0,2:T(2,128)(2,1)} %copy.89), calls=%async_computation | async-start | bytes 4194304 | tf_op jit(solution)/shard_map/all_to_all | solution.py:77
  21.0 98.3 %all-gather.5.cloned.1.call-start = ((), (), s32[]{:S(2)}) async-start(), calls=%async_computation.2 | async-start | bytes 1671168 | tf_op jit(solution)/shard_map/all_gather | solution.py:13
  71.2 2.2 copy-start.4
  71.2 2.8 copy-start.3
  73.3 201.0 %reduce-scatter.4.cloned.1.call-start = ((), (), s32[]{:S(2)}) async-start(), calls=%async_computation.3 | async-start | bytes 3538944
  153.1 8.3 %copy-start.5 = (bf16[4,768]{1,0:T(4,128)(2,1)S(1)}, bf16[4,768]{1,0:T(4,128)(2,1)}, u32[]{:S(2)}) copy-start(bf16[4,768]{1,0:T(4,128)(2,1)} %param.14) | copy-start | bytes 18436
  153.1 39.4 %copy-start.8 = (bf16[6144,4]{0,1:T(4,128)(2,1)S(1)}, bf16[6144,4]{0,1:T(4,128)(2,1)}, u32[]{:S(2)}) copy-start(bf16[6144,4]{0,1:T(4,128)(2,1)} %param.22) | copy-start | bytes 147460
  153.1 39.6 %copy-start.6 = (s32[4,2]{0,1:T(2,128)S(1)}, s32[4,2]{0,1:T(2,128)}, u32[]{:S(2)}) copy-start(s32[4,2]{0,1:T(2,128)} %param.19) | copy-start | bytes 100
  154.9 40.5 %copy-start.7 = (f32[4,2]{0,1:T(2,128)S(1)}, f32[4,2]{0,1:T(2,128)}, u32[]{:S(2)}) copy-start(f32[4,2]{0,1:T(2,128)} %compare_convert_fusion) | copy-start | bytes 100
  161.4 39.9 %copy-start.2 = (bf16[4,768]{1,0:T(4,128)(2,1)}, bf16[4,768]{1,0:T(4,128)(2,1)S(1)}, u32[]{:S(2)}) copy-start(bf16[4,768]{1,0:T(4,128)(2,1)S(1)} %add_convert_fusion) | copy-start | bytes 18436
Sparse Core Ops, SparseCore 0:
  73.4 39.7 all-gather.4
  201.5 72.7 reduce-scatter.3
where the time goes:
time: 288 us; the launch traced here: 286 us
  waiting for transfers between devices  119 us (41%)
  blocking collectives  78.8 us (27%)
  local copies, waits for them, and re-layouts  35.9 us (12%)
  other arithmetic  16.7 us (6%)
  between operations  14.3 us (5%)
  matrix products  13.4 us (5%)
  starting transfers between devices  7.52 us (3%)
    unnamed x3, waiting for transfers between devices  72.9 us
    all_to_all x1, waiting for transfers between devices, on_device(): lax.all_to_all(kv_cache, 'seq', split_axis=2, concat_axis=1, tiled=True)  46.3 us
    all_gather x2, blocking collectives, combined_all(): pieces = jax.tree.map(lambda part: lax.all_gather(part, axis), value)  38.9 us
    all_gather x1, blocking collectives, on_device(): gathered = lax.all_gather(attended, 'seq', axis=1, tiled=True)  30.8 us
    dynamic_slice x15, local copies, waits for them, and re-layouts, combined_all(): lax.scan(lambda running, share: (join(running, share), None), head, tail)  13.5 us
    add x15, other arithmetic, merge_parts(): total_left * scale_left + total_right * scale_right  11.2 us
    unnamed x22, local copies, waits for them, and re-layouts  7.55 us
    all_to_all x1, starting transfers between devices, on_device(): lax.all_to_all(kv_cache, 'seq', split_axis=2, concat_axis=1, tiled=True)  7.44 us
  transfers between devices with their start and end apart: 3, of which 2 were waited for; matrix products, arithmetic and copies ran while one was open for 2% of the time, Pallas kernels for 0%

commit v1 on v0

--- a/solution.py
+++ b/solution.py
@@ -66,6 +66,13 @@
     w_up,
     w_down,
 ):
+
+    def use_axis_part_up(array_here, dim_k, where_dim):
+        b_next = jax.lax.all_to_all(
+            jnp.stack(jnp.split(array_here, jax.lax.axis_size("seq"), dim_k), axis=0), "seq", 0, 0
+        )
+        return jnp.concatenate(b_next, where_dim)
+
     requests = lengths.shape[0]
     seq_count = lax.axis_size("seq")
     core_count = lax.axis_size("expert")
@@ -74,7 +81,7 @@
     half_ctx = kv_cache.shape[2] // requests
     ctx_dev = half_ctx // seq_count
     own_heads = KVH // core_count
-    relaid = lax.all_to_all(kv_cache, "seq", split_axis=2, concat_axis=1, tiled=True)
+    relaid = use_axis_part_up(kv_cache, 2, 1)
     positions = core_index * half_ctx + seq_index * ctx_dev + jnp.arange(ctx_dev, dtype=jnp.int32)
     all_queries = lax.all_gather(queries, "expert", axis=1, tiled=True)
     partials = partial_attention(all_queries, relaid, positions, lengths, KVH)

time: 288 us -> 304 us (1.056)
  local copies, waits for them, and re-layouts: 35.9 us -> 49 us
    unnamed x22 -> x28, local copies, waits for them, and re-layouts: 7.55 us -> 13.1 us
    slice x1 -> x2, local copies, waits for them, and re-layouts: 0.19 us -> 5.47 us  [partial_attention(): value_rows = relaid[1].reshape(kv_count, HD, slot_count, requests)]
where the time goes in v1:
time: 304 us; the launch traced here: 302 us
  waiting for transfers between devices  119 us (39%)
  blocking collectives  79 us (26%)
  local copies, waits for them, and re-layouts  49 us (16%)
  other arithmetic  16.7 us (5%)
  matrix products  15.9 us (5%)
  between operations  14.3 us (5%)
  starting transfers between devices  7.52 us (2%)
    unnamed x3, waiting for transfers between devices  73 us
    all_to_all x1, waiting for transfers between devices, use_axis_part_up(): jax.lax.all_to_all(jnp.stack(jnp.split(array_here, jax.lax.axis_size('seq...  46.3 us
    all_gather x2, blocking collectives, combined_all(): pieces = jax.tree.map(lambda part: lax.all_gather(part, axis), value)  38.9 us
    all_gather x1, blocking collectives, on_device(): gathered = lax.all_gather(attended, 'seq', axis=1, tiled=True)  30.8 us
    dynamic_slice x15, local copies, waits for them, and re-layouts, combined_all(): lax.scan(lambda running, share: (join(running, share), None), head, tail)  13.5 us
    unnamed x28, local copies, waits for them, and re-layouts  13.1 us
    add x15, other arithmetic, merge_parts(): total_left * scale_left + total_right * scale_right  11.2 us
    all_to_all x1, starting transfers between devices, use_axis_part_up(): jax.lax.all_to_all(jnp.stack(jnp.split(array_here, jax.lax.axis_size('seq...  7.44 us
  transfers between devices with their start and end apart: 3, of which 2 were waited for; matrix products, arithmetic and copies ran while one was open for 2% of the time, Pallas kernels for 0%

profile of v1, /device:TPU:0, one launch (start us, length us, event | category | flops | bytes accessed | tf_op | source)
XLA Modules:
  0.0 301.9 jit_solution(11657298042880161934)
XLA Ops:
  7.2 1.8 bitcast_dynamic-update-slice_fusion.7
  9.0 1.7 bitcast_dynamic-update-slice_fusion.6
  10.7 1.7 bitcast_dynamic-update-slice_fusion.5
  12.4 1.7 bitcast_dynamic-update-slice_fusion.4
  14.0 1.7 bitcast_dynamic-update-slice_fusion.3
  15.7 1.7 bitcast_dynamic-update-slice_fusion.2
  17.4 1.7 bitcast_dynamic-update-slice_fusion.1
  19.1 1.7 bitcast_dynamic-update-slice_fusion
  20.7 7.4 %all-to-all-start = ((bf16[8,2,128,512]{3,2,1,0:T(8,128)(2,1)}), bf16[8,2,128,512]{3,2,1,0:T(8,128)(2,1)}, u32[]{:S(2)}, u32[]{:S(2)}) async-start(bf16[8,2,128,512]{3,2,1,0:T(8,128)(2,1)} %bitcast_dynamic-update-slice_fusion), calls=%async_computation | async-start | bytes 4194304 | tf_op jit(solution)/shard_map/all_to_all | solution.py:71
  28.3 1.8 all_gather.24
  30.3 46.3 %all-to-all-done = bf16[8,2,128,512]{3,2,1,0:T(8,128)(2,1)} async-done(((bf16[8,2,128,512]{3,2,1,0:T(8,128)(2,1)}), bf16[8,2,128,512]{3,2,1,0:T(8,128)(2,1)}, u32[]{:S(2)}, u32[]{:S(2)}) %all-to-all-start) | async-done | bytes 2097184 | tf_op jit(solution)/shard_map/all_to_all | solution.py:71
  76.5 3.0 %fusion.31 = (bf16[1,8,128,512]{3,2,0,1:T(8,128)(2,1)}, bf16[1,8,128,512]{3,2,0,1:T(8,128)(2,1)}) fusion(bf16[2,8,128,512]{3,2,0,1:T(8,128)(2,1)} %bitcast.11), kind=kLoop, calls=%fused_computation.69 | loop fusion | bytes 4194304 | tf_op jit(solution)/shard_map/slice | solution.py:39
  79.6 2.4 copy.92
  82.0 2.4 copy.94
  84.5 2.0 select_reduce_fusion
  86.4 1.7 fusion.6
  91.2 20.3 %all-gather.1 = f32[64,8,6]{2,1,0:T(8,128)S(1)} all-gather(f32[4,8,6]{2,1,0:T(8,128)S(1)} %bitcast_reduce_fusion), channel_id=3, replica_groups=mesh['groups'=2,'seq'=8,'expert'=2] {'seq','expert'}, dimensions={0}, use_global_device_ids=true | all-gather | bytes 13056 | tf_op jit(solution)/shard_map/all_gather | solution.py:13
  111.5 18.6 %all-gather = f32[64,8,6]{2,1,0:T(8,128)S(1)} all-gather(f32[4,8,6]{2,1,0:T(8,128)S(1)} %get-tuple-element.106), channel_id=2, replica_groups=mesh['groups'=2,'seq'=8,'expert'=2] {'seq','expert'}, dimensions={0}, use_global_device_ids=true | all-gather | bytes 13056 | tf_op jit(solution)/shard_map/all_gather | solution.py:13
  131.4 1.1 copy.103
  132.6 1.4 copy.102
  134.8 0.9 slice.60
  135.7 2.6 slice.63
  138.3 30.3 %while.14 = (s32[]{:T(128)}, f32[4,8,6]{1,0,2:T(4,128)S(1)}, f32[4,8,6]{1,0,2:T(4,128)S(1)}, f32[4,8,6,128]{3,2,1,0:T(8,128)S(1)}, f32[15,4,8,6]{2,1,3,0:T(4,128...) while((s32[]{:T(128)}, f32[4,8,6]{1,0,2:T(4,128)S(1)}, ...), condition=%wide.region_3.4_spmd, body=%wide.region_2.3_spmd.sunk | while | flops 74882 | bytes 502365 | solution.py:16
  141.3 0.9 constant_dynamic-slice_fusion.2
  170.5 3.1 %fusion.33 = f32[4,768]{1,0:T(4,128)S(1)} fusion(bf16[4,3072]{1,0:T(4,128)(2,1)S(1)} %convert_element_type.53, bf16[3072,768]{1,0:T(8,128)(2,1)} %param.20), kind=kOutput, calls=%fused_computation.71 | convolution fusion | flops 18874368 | bytes 4755456 | tf_op jit(solution)/shard_map/dot_general | solution.py:110
  173.5 3.6 %psum.14 = f32[4,768]{1,0:T(4,128)S(1)} all-reduce(f32[4,768]{1,0:T(4,128)S(1)} %fusion.33), channel_id=1, replica_groups=mesh['groups'=2,'seq'=8,'expert'=2] {'expert'}, use_global_device_ids=true, to_apply=%region_4.5 | all-reduce | flops 3072 | bytes 24576 | tf_op jit(solution)/shard_map/psum | solution.py:111
  177.2 30.8 %all_gather.31 = bf16[4,6144]{1,0:T(4,128)(2,1)S(1)} all-gather(bf16[4,768]{1,0:T(4,128)(2,1)S(1)} %add_convert_fusion), channel_id=1, replica_groups=mesh['groups'=2,'seq'=8,'expert'=2] {'seq'}, dimensions={1}, use_global_device_ids=true | all-gather | bytes 55296 | tf_op jit(solution)/shard_map/all_gather | solution.py:112
  208.7 2.4 fusion.17
  211.2 5.8 %convolution_bitcast_fusion = f32[6144,4]{1,0:T(8,128)} fusion(bf16[2,128,6144]{2,1,0:T(8,128)(2,1)S(1)} %copy-done, bf16[2,6144,128]{2,1,0:T(8,128)(2,1)} %param.24, bf16[4,6144]{1,0:T(4,128)(2,1)S(1)} %fusion.11, f32[4,2,128]{2,0,1:T(4,128)S(1)} %fusion.17, f32[4,2]{0,1:T(2,128)S(1)} %multiply_reduce_fusion), kind=kOutput, calls=%fused_computation.10 | convolution fusion | flops 25172992 | bytes 6443040 | tf_op jit(solution)/shard_map/ref,efd->rd/dot_general | solution.py:135
  217.1 72.9 %reduce-scatter.4.cloned.1.call-done = f32[768,4]{1,0:T(8,128)} async-done(((f32[6144,4]{1,0:T(8,128)}), f32[768,4]{1,0:T(8,128)}) %reduce-scatter.4.cloned.1.call-update) | async-done | bytes 12304
  290.0 1.1 copy.114
  291.1 3.9 %psum.15 = bf16[4,768]{1,0:T(4,128)(2,1)} all-reduce(f32[4,768]{1,0:T(4,128)S(1)} %copy.114), channel_id=1, replica_groups=mesh['groups'=2,'seq'=8,'expert'=2] {'expert'}, use_global_device_ids=true, to_apply=%region_10.11 | all-reduce | flops 3072 | bytes 18432 | tf_op jit(solution)/shard_map/psum | solution.py:137
  (134 shorter events, 37.2 us)
Async XLA Ops:
  7.2 204.0 %copy-start = (bf16[2,128,6144]{2,1,0:T(8,128)(2,1)S(1)}, bf16[2,128,6144]{2,1,0:T(8,128)(2,1)}, u32[]{:S(2)}) copy-start(bf16[2,128,6144]{2,1,0:T(8,128)(2,1)} %param.25) | copy-start | bytes 9437188
  20.7 7.5 %copy-start.1 = (bf16[4,3072]{1,0:T(4,128)(2,1)S(1)}, bf16[4,3072]{1,0:T(4,128)(2,1)}, u32[]{:S(2)}) copy-start(bf16[4,3072]{1,0:T(4,128)(2,1)} %param.15) | copy-start | bytes 73732
  20.7 9.4 %copy-start.9 = (s32[4]{0:T(128)S(1)}, s32[4]{0:T(128)}, u32[]{:S(2)}) copy-start(s32[4]{0:T(128)} %param.18) | copy-start | bytes 52
  20.7 55.8 %all-to-all-start = ((bf16[8,2,128,512]{3,2,1,0:T(8,128)(2,1)}), bf16[8,2,128,512]{3,2,1,0:T(8,128)(2,1)}, u32[]{:S(2)}, u32[]{:S(2)}) async-start(bf16[8,2,128,512]{3,2,1,0:T(8,128)(2,1)} %bitcast_dynamic-update-slice_fusion), calls=%async_computation | async-start | bytes 4194304 | tf_op jit(solution)/shard_map/all_to_all | solution.py:71
  28.2 106.6 %all-gather.5.cloned.1.call-start = ((), (), s32[]{:S(2)}) async-start(), calls=%async_computation.2 | async-start | bytes 1671168 | tf_op jit(solution)/shard_map/all_gather | solution.py:13
  84.4 4.5 %copy-start.4 = (bf16[2,4,512]{2,1,0:T(4,128)(2,1)S(1)}, bf16[2,4,512]{2,1,0:T(4,128)(2,1)}, u32[]{:S(2)}) copy-start(bf16[2,4,512]{2,1,0:T(4,128)(2,1)} %param.16) | copy-start | bytes 24580
  84.4 5.1 %copy-start.3 = (bf16[6144]{0:T(1024)(128)(2,1)S(1)}, bf16[6144]{0:T(1024)(128)(2,1)}, u32[]{:S(2)}) copy-start(bf16[6144]{0:T(1024)(128)(2,1)} %param.21) | copy-start | bytes 36868
  88.8 201.2 %reduce-scatter.4.cloned.1.call-start = ((), (), s32[]{:S(2)}) async-start(), calls=%async_computation.3 | async-start | bytes 3538944
  170.4 6.7 %copy-start.5 = (bf16[4,768]{1,0:T(4,128)(2,1)S(1)}, bf16[4,768]{1,0:T(4,128)(2,1)}, u32[]{:S(2)}) copy-start(bf16[4,768]{1,0:T(4,128)(2,1)} %param.14) | copy-start | bytes 18436
  170.4 37.8 %copy-start.8 = (bf16[6144,4]{0,1:T(4,128)(2,1)S(1)}, bf16[6144,4]{0,1:T(4,128)(2,1)}, u32[]{:S(2)}) copy-start(bf16[6144,4]{0,1:T(4,128)(2,1)} %param.22) | copy-start | bytes 147460
  170.5 37.9 %copy-start.6 = (s32[4,2]{0,1:T(2,128)S(1)}, s32[4,2]{0,1:T(2,128)}, u32[]{:S(2)}) copy-start(s32[4,2]{0,1:T(2,128)} %param.19) | copy-start | bytes 100
  173.5 37.5 %copy-start.7 = (f32[4,2]{0,1:T(2,128)S(1)}, f32[4,2]{0,1:T(2,128)}, u32[]{:S(2)}) copy-start(f32[4,2]{0,1:T(2,128)} %compare_convert_fusion) | copy-start | bytes 100
  177.2 39.9 %copy-start.2 = (bf16[4,768]{1,0:T(4,128)(2,1)}, bf16[4,768]{1,0:T(4,128)(2,1)S(1)}, u32[]{:S(2)}) copy-start(bf16[4,768]{1,0:T(4,128)(2,1)S(1)} %add_convert_fusion) | copy-start | bytes 18436
Sparse Core Ops, SparseCore 0:
  89.0 39.7 all-gather.4
  217.2 72.7 reduce-scatter.3
